TPU v7x, 32 devices: a whole 2x2x4 slice. The times are simulated.
32 devices in a mesh: bank: 8 (over y, x, core), zero: 4 (over z).
Axes of the slice: x: 2, y: 2, z: 4, core: 2. Of those that a mesh axis runs over, the one named last changes fastest.
Arguments:
- master_down: float32 [64, 1024, 2048], P('bank', None, 'zero'), may hold values from -0.25 to 0.25
- router_weight: float32 [2048, 64], P('zero', 'bank'), may hold values from -0.125 to 0.125
- router_gain: float32 [2048], P('zero'), may hold values from 0.25 to 1.75
Outputs:
- final_down: bfloat16 [64, 1024, 2048], P('bank')
- scale_down: float32 [64, 1024], P('bank')
- serve_router: bfloat16 [2048, 64], replicated
All inputs are finite; a program needn't handle non-finite values. Where the computation divides by a largest or mean magnitude, that divisor is 1e-20 or more.
Results may differ from a plain program's by a relative error of at most 0.001.
Values may be sent and summed in bfloat16 or wider, within the bound.
A program may use at most 128 MiB of HBM per device.

v0:
```python
import jax
import jax.numpy as jnp
from jax import lax
from jax.sharding import PartitionSpec as P


def per_device(master_down, router_weight, router_gain):
    scale_down = lax.pmax(jnp.max(jnp.abs(master_down), axis=2), "zero")
    narrow_down = (master_down / jnp.expand_dims(scale_down, 2)).astype(jnp.bfloat16)
    final_down = lax.all_gather(narrow_down, "zero", axis=2, tiled=True)
    part_router = (router_weight * router_gain[:, None]).astype(jnp.bfloat16)
    row_router = lax.all_gather(part_router, "zero", axis=0, tiled=True)
    serve_router = lax.all_gather(row_router, "bank", axis=1, tiled=True)
    return (final_down, scale_down, serve_router)


def solution(mesh):
    placed = (P("bank", None, "zero"), P("zero", "bank"), P("zero"))
    return jax.shard_map(
        per_device,
        mesh=mesh,
        in_specs=placed,
        out_specs=(P("bank", None, None), P("bank", None), P()),
        check_vma=False,
    )
```

profile of v0, /device:TPU:0, one launch (start us, length us, event | category | flops | bytes accessed | tf_op | source)
XLA Modules:
  0.0 634.6 jit_solution(17249483322936477532)
XLA Ops:
  7.2 0.0 all-gather.2.cloned.1.call-start
  7.2 7.1 %abs_reduce_fusion = f32[8,1024]{1,0:T(8,128)S(1)} fusion(f32[8,1024,512]{2,1,0:T(8,128)} %param.3), kind=kLoop, calls=%fused_computation.1 | loop fusion | flops 8380416 | bytes 16809984 | tf_op jit(solution)/shard_map/reduce_max | solution.py:8
  14.3 20.8 %pmax.7 = f32[8,1024]{1,0:T(8,128)S(1)} all-reduce(f32[8,1024]{1,0:T(8,128)S(1)} %abs_reduce_fusion), channel_id=1, replica_groups=mesh['bank'=8,'zero'=4] {'zero'}, use_global_device_ids=true, to_apply=%region_1.0 | all-reduce | flops 8192 | bytes 65536 | tf_op jit(solution)/shard_map/pmax | solution.py:8
  35.1 0.0 copy-start
  35.1 0.0 copy-start.1
  35.2 0.0 copy-start.2
  35.2 9.2 %divide_convert_fusion = bf16[8,1024,512]{2,1,0:T(8,128)(2,1)} fusion(f32[8,1024,512]{2,1,0:T(8,128)} %param.3, f32[8,1024]{1,0:T(8,128)S(1)} %pmax.7), kind=kLoop, calls=%fused_computation | loop fusion | flops 8388608 | bytes 25198592 | tf_op jit(solution)/shard_map/convert_element_type | solution.py:9
  44.3 0.0 all-gather.2.cloned.1.call-update
  44.4 0.0 copy-done
  44.4 0.0 copy-done.1
  44.4 0.0 copy-done.2
  44.4 13.1 %all_gather.10 = bf16[2048,8]{0,1:T(8,128)(2,1)S(1)} all-gather(bf16[512,8]{0,1:T(8,128)(2,1)S(1)} %multiply_convert_fusion), channel_id=1, replica_groups=mesh['bank'=8,'zero'=4] {'zero'}, dimensions={0}, use_global_device_ids=true | all-gather | bytes 40960 | tf_op jit(solution)/shard_map/all_gather | solution.py:12
  57.5 9.3 %all_gather.11 = bf16[2048,64]{0,1:T(8,128)(2,1)S(1)} all-gather(bf16[2048,8]{0,1:T(8,128)(2,1)S(1)} %all_gather.10), channel_id=1, replica_groups=mesh['bank'=8,'zero'=4] {'bank'}, dimensions={1}, use_global_device_ids=true | all-gather | bytes 294912 | tf_op jit(solution)/shard_map/all_gather | solution.py:13
  66.8 537.3 %all-gather.2.cloned.1.call-done = bf16[8,1024,2048]{2,1,0:T(8,128)(2,1)} async-done(((bf16[8,1024,512]{2,1,0:T(8,128)(2,1)}), bf16[8,1024,2048]{2,1,0:T(8,128)(2,1)}) %all-gather.2.cloned.1.call-update) | async-done | bytes 33554448 | tf_op jit(solution)/shard_map/all_gather | solution.py:10
  604.1 22.9 %copy.8 = bf16[8,1024,2048]{2,1,0:T(8,128)(2,1)} copy(bf16[8,1024,2048]{2,1,0:T(8,128)(2,1)} %all-gather.2.cloned.1.call-done) | data formatting | bytes 67108864
  627.0 0.7 copy.9
  (1 shorter events, 0.0 us)
Async XLA Ops:
  7.2 597.0 %all-gather.2.cloned.1.call-start = ((), (), s32[]{:S(2)}) async-start(), calls=%async_computation | async-start | bytes 41943040 | tf_op jit(solution)/shard_map/all_gather | solution.py:10
  35.1 9.2 %copy-start = (f32[8,1024]{1,0:T(8,128)}, f32[8,1024]{1,0:T(8,128)S(1)}, u32[]{:S(2)}) copy-start(f32[8,1024]{1,0:T(8,128)S(1)} %pmax.7) | copy-start | bytes 98308
  35.1 9.2 %copy-start.1 = (f32[512,8]{0,1:T(8,128)S(1)}, f32[512,8]{0,1:T(8,128)}, u32[]{:S(2)}) copy-start(f32[512,8]{0,1:T(8,128)} %param.4) | copy-start | bytes 49156
  35.2 9.2 %copy-start.2 = (f32[512]{0:T(512)S(1)}, f32[512]{0:T(512)}, u32[]{:S(2)}) copy-start(f32[512]{0:T(512)} %param.5) | copy-start | bytes 6148
Sparse Core Ops, SparseCore 0:
  44.5 559.6 all-gather.1
where the time goes:
time: 635 us
  waiting for transfers between devices  537 us (85%)
  blocking collectives  43.2 us (7%)
  local copies, waits for them, and re-layouts  23.6 us (4%)
  other arithmetic  16.3 us (3%)
  between operations  14.1 us (2%)
    all_gather x1, waiting for transfers between devices, per_device(): final_down = lax.all_gather(narrow_down, 'zero', axis=2, tiled=True)  537 us
    unnamed x8, local copies, waits for them, and re-layouts  23.6 us
    pmax x1, blocking collectives, per_device(): scale_down = lax.pmax(jnp.max(jnp.abs(master_down), axis=2), 'zero')  20.8 us
    all_gather x1, blocking collectives, per_device(): row_router = lax.all_gather(part_router, 'zero', axis=0, tiled=True)  13.1 us
  transfers between devices with their start and end apart: 1, of which 1 were waited for; matrix products, arithmetic and copies ran while one was open for 0% of the time, Pallas kernels for 0%

commit v1 on v0

--- a/solution.py
+++ b/solution.py
@@ -7,7 +7,8 @@
 def per_device(master_down, router_weight, router_gain):
     scale_down = lax.pmax(jnp.max(jnp.abs(master_down), axis=2), "zero")
     narrow_down = (master_down / jnp.expand_dims(scale_down, 2)).astype(jnp.bfloat16)
-    final_down = lax.all_gather(narrow_down, "zero", axis=2, tiled=True)
+    blocks = lax.all_gather(narrow_down, "zero", axis=0, tiled=False)
+    final_down = jnp.concatenate(blocks, axis=2)
     part_router = (router_weight * router_gain[:, None]).astype(jnp.bfloat16)
     row_router = lax.all_gather(part_router, "zero", axis=0, tiled=True)
     serve_router = lax.all_gather(row_router, "bank", axis=1, tiled=True)

time: 635 us -> 635 us (level)
    unnamed x8 -> x7, local copies, waits for them, and re-layouts: 23.6 us -> 0.72 us
    reshape x0 -> x1, local copies, waits for them, and re-layouts: none -> 22.8 us  [per_device(): final_down = jnp.concatenate(blocks, axis=2)]
where the time goes in v1:
time: 635 us
  waiting for transfers between devices  537 us (85%)
  blocking collectives  43.2 us (7%)
  local copies, waits for them, and re-layouts  23.5 us (4%)
  other arithmetic  16.3 us (3%)
  between operations  14.1 us (2%)
    all_gather x1, waiting for transfers between devices, per_device(): blocks = lax.all_gather(narrow_down, 'zero', axis=0, tiled=False)  537 us
    reshape x1, local copies, waits for them, and re-layouts, per_device(): final_down = jnp.concatenate(blocks, axis=2)  22.8 us
    pmax x1, blocking collectives, per_device(): scale_down = lax.pmax(jnp.max(jnp.abs(master_down), axis=2), 'zero')  20.8 us
    all_gather x1, blocking collectives, per_device(): row_router = lax.all_gather(part_router, 'zero', axis=0, tiled=True)  13.1 us
  transfers between devices with their start and end apart: 1, of which 1 were waited for; matrix products, arithmetic and copies ran while one was open for 0% of the time, Pallas kernels for 0%

profile of v1, /device:TPU:0, one launch (start us, length us, event | category | flops | bytes accessed | tf_op | source)
XLA Modules:
  0.0 634.5 jit_solution(10776684073163324914)
XLA Ops:
  7.2 0.0 all-gather.3.cloned.1.call-start
  7.2 7.1 %abs_reduce_fusion = f32[8,1024]{1,0:T(8,128)S(1)} fusion(f32[8,1024,512]{2,1,0:T(8,128)} %param.3), kind=kLoop, calls=%fused_computation.1 | loop fusion | flops 8380416 | bytes 16809984 | tf_op jit(solution)/shard_map/reduce_max | solution.py:8
  14.3 20.8 %pmax.7 = f32[8,1024]{1,0:T(8,128)S(1)} all-reduce(f32[8,1024]{1,0:T(8,128)S(1)} %abs_reduce_fusion), channel_id=1, replica_groups=mesh['bank'=8,'zero'=4] {'zero'}, use_global_device_ids=true, to_apply=%region_1.0 | all-reduce | flops 8192 | bytes 65536 | tf_op jit(solution)/shard_map/pmax | solution.py:8
  35.1 0.0 copy-start
  35.1 0.0 copy-start.1
  35.2 0.0 copy-start.2
  35.2 9.2 %divide_convert_fusion = bf16[8,1024,512]{2,1,0:T(8,128)(2,1)} fusion(f32[8,1024,512]{2,1,0:T(8,128)} %param.3, f32[8,1024]{1,0:T(8,128)S(1)} %pmax.7), kind=kLoop, calls=%fused_computation | loop fusion | flops 8388608 | bytes 25198592 | tf_op jit(solution)/shard_map/convert_element_type | solution.py:9
  44.3 0.0 all-gather.3.cloned.1.call-update
  44.4 0.0 copy-done
  44.4 0.0 copy-done.1
  44.4 0.0 copy-done.2
  44.4 13.1 %all_gather.14 = bf16[2048,8]{0,1:T(8,128)(2,1)S(1)} all-gather(bf16[512,8]{0,1:T(8,128)(2,1)S(1)} %multiply_convert_fusion), channel_id=1, replica_groups=mesh['bank'=8,'zero'=4] {'zero'}, dimensions={0}, use_global_device_ids=true | all-gather | bytes 40960 | tf_op jit(solution)/shard_map/all_gather | solution.py:13
  57.5 9.3 %all_gather.15 = bf16[2048,64]{0,1:T(8,128)(2,1)S(1)} all-gather(bf16[2048,8]{0,1:T(8,128)(2,1)S(1)} %all_gather.14), channel_id=1, replica_groups=mesh['bank'=8,'zero'=4] {'bank'}, dimensions={1}, use_global_device_ids=true | all-gather | bytes 294912 | tf_op jit(solution)/shard_map/all_gather | solution.py:14
  66.8 537.3 %all-gather.3.cloned.1.call-done = bf16[32,1024,512]{2,1,0:T(8,128)(2,1)} async-done(((bf16[8,1024,512]{2,1,0:T(8,128)(2,1)}), bf16[32,1024,512]{2,1,0:T(8,128)(2,1)}) %all-gather.3.cloned.1.call-update) | async-done | bytes 33554448 | tf_op jit(solution)/shard_map/all_gather | solution.py:10
  604.1 22.8 %copy.8 = bf16[4,8,128,8,512]{4,3,0,2,1:T(8,128)(2,1)} copy(bf16[4,8,128,8,512]{4,3,2,1,0:T(8,128)(2,1)} %bitcast.5) | data formatting | bytes 67108864 | tf_op jit(solution)/shard_map/reshape | solution.py:11
  627.0 0.7 copy.10
  (1 shorter events, 0.0 us)
Async XLA Ops:
  7.2 597.0 %all-gather.3.cloned.1.call-start = ((), (), s32[]{:S(2)}) async-start(), calls=%async_computation | async-start | bytes 41943040 | tf_op jit(solution)/shard_map/all_gather | solution.py:10
  35.1 9.2 %copy-start = (f32[8,1024]{1,0:T(8,128)}, f32[8,1024]{1,0:T(8,128)S(1)}, u32[]{:S(2)}) copy-start(f32[8,1024]{1,0:T(8,128)S(1)} %pmax.7) | copy-start | bytes 98308
  35.1 9.2 %copy-start.1 = (f32[512,8]{0,1:T(8,128)S(1)}, f32[512,8]{0,1:T(8,128)}, u32[]{:S(2)}) copy-start(f32[512,8]{0,1:T(8,128)} %param.4) | copy-start | bytes 49156
  35.2 9.2 %copy-start.2 = (f32[512]{0:T(512)S(1)}, f32[512]{0:T(512)}, u32[]{:S(2)}) copy-start(f32[512]{0:T(512)} %param.5) | copy-start | bytes 6148
Sparse Core Ops, SparseCore 0:
  44.5 559.6 all-gather.2
